TPU v7x, 32 devices: a whole 2x2x4 slice. The times are simulated.
32 devices in a mesh: shard: 8 (over z, y), tp: 4 (over x, core).
Axes of the slice: x: 2, y: 2, z: 4, core: 2. Of those that a mesh axis runs over, the one named last changes fastest.
Arguments:
- gradient: bfloat16 [4096, 16384], P('shard', 'tp'), may hold values from -2 to 2
- table: int32 [256, 3], replicated, may hold values from 0 to 31, as said below
- left_stat: bfloat16 [384, 512, 512], P(('shard', 'tp')), as said below
- right_stat: bfloat16 [384, 512, 512], P(('shard', 'tp')), as said below
- left_basis: bfloat16 [384, 512, 512], P(('shard', 'tp')), may hold values from -0.25 to 0.25
- right_basis: bfloat16 [384, 512, 512], P(('shard', 'tp')), may hold values from -0.25 to 0.25
- moment: bfloat16 [384, 512, 512], P(('shard', 'tp')), may hold values from -2 to 2
- second: float32 [384, 512, 512], P(('shard', 'tp')), may hold values from 0.02 to 0.2
Outputs:
- update: bfloat16 [4096, 16384], P('shard', 'tp')
- new_left: bfloat16 [384, 512, 512], P(('shard', 'tp'))
- new_right: bfloat16 [384, 512, 512], P(('shard', 'tp'))
- new_moment: bfloat16 [384, 512, 512], P(('shard', 'tp'))
- new_second: float32 [384, 512, 512], P(('shard', 'tp'))
Inputs may be any that keep to these rules, and one draw needn't show every extreme that they name: `table`: column 0 is a block row below 8, column 1 a block column below 32, column 2 an owner device below 32; every block appears in exactly one row; each device owns between 4 and 12 blocks, and some device owns exactly 12. `left_stat`: Symmetric. `right_stat`: Symmetric.
All inputs are finite; a program needn't handle non-finite values.
Results may differ from a plain program's by a relative error of at most 0.0085.
Values may be sent and summed in bfloat16 or wider, within the bound.
A program may use at most 192 MiB of HBM per device.

v0:
```python
import jax
import jax.numpy as jnp
from jax import lax
from jax.sharding import PartitionSpec as P

beta_moment = 0.9
beta_second = 0.95
beta_stats = 0.95
epsilon = 1e-08


def slot_table(table, slots):
    owners = table[:, 2]
    count = owners.shape[0]
    order = jnp.arange(count, dtype=jnp.int32)
    earlier = (owners[None, :] == owners[:, None]) & (order[None, :] < order[:, None])
    slot_rank = jnp.sum(earlier.astype(jnp.int32), axis=1)
    return owners * slots + slot_rank


def move_grad(array):
    return lax.all_to_all(array, ("shard", "tp"), split_axis=1, concat_axis=1, tiled=True)


def move_blocks(array):
    return lax.all_to_all(array, ("shard", "tp"), split_axis=2, concat_axis=2, tiled=True)


def move_updates(array):
    return lax.all_to_all(array, ("shard", "tp"), split_axis=2, concat_axis=2, tiled=True)


def move_stripes(array):
    return lax.all_to_all(array, ("shard", "tp"), split_axis=1, concat_axis=1, tiled=True)


def precondition_slots(grad_blocks, left, right, left_q, right_q, first, squares):
    left_new = (
        beta_stats * left.astype(jnp.float32)
        + (1.0 - beta_stats)
        * jnp.einsum("sik,sjk->sij", grad_blocks, grad_blocks, preferred_element_type=jnp.float32)
    ).astype(jnp.bfloat16)
    right_new = (
        beta_stats * right.astype(jnp.float32)
        + (1.0 - beta_stats)
        * jnp.einsum("ski,skj->sij", grad_blocks, grad_blocks, preferred_element_type=jnp.float32)
    ).astype(jnp.bfloat16)
    first_new = (
        beta_moment * first.astype(jnp.float32)
        + (1.0 - beta_moment) * grad_blocks.astype(jnp.float32)
    ).astype(jnp.bfloat16)
    left_grad = jnp.einsum(
        "ski,skj->sij", left_q, grad_blocks, preferred_element_type=jnp.float32
    ).astype(jnp.bfloat16)
    left_first = jnp.einsum(
        "ski,skj->sij", left_q, first_new, preferred_element_type=jnp.float32
    ).astype(jnp.bfloat16)
    rotated = jnp.einsum("sij,sjk->sik", left_grad, right_q, preferred_element_type=jnp.float32)
    first_rot = jnp.einsum("sij,sjk->sik", left_first, right_q, preferred_element_type=jnp.float32)
    squares_new = beta_second * squares + (1.0 - beta_second) * rotated * rotated
    scaled = (first_rot / (jnp.sqrt(squares_new) + epsilon)).astype(jnp.bfloat16)
    back = jnp.einsum("sij,sjk->sik", left_q, scaled, preferred_element_type=jnp.float32).astype(
        jnp.bfloat16
    )
    result = jnp.einsum("sij,skj->sik", back, right_q, preferred_element_type=jnp.float32).astype(
        jnp.bfloat16
    )
    return (result, left_new, right_new, first_new, squares_new)


def shards(gradient, table, left_stat, right_stat, left_basis, right_basis, moment, second):
    shard_count = lax.axis_size("shard")
    tp_count = lax.axis_size("tp")
    dev_count = shard_count * tp_count
    row_dev, col_dev = gradient.shape
    slots = left_stat.shape[0]
    side = left_stat.shape[1]
    halves = side // row_dev
    block_rows = shard_count // halves
    cols_per_dev = col_dev // side
    block_cols = tp_count * cols_per_dev
    piece_len = row_dev * side // dev_count
    tiled = gradient.reshape(row_dev, cols_per_dev, side).transpose(1, 0, 2)
    received = move_grad(tiled.reshape(cols_per_dev, dev_count, piece_len))
    spread = received.reshape(cols_per_dev, block_rows, halves, tp_count, piece_len)
    state_row = slot_table(table, slots)
    block_id = table[:, 0] * block_cols + table[:, 1]
    targets = jnp.arange(dev_count * slots, dtype=jnp.int32)
    matches = (state_row[None, :] == targets[:, None]).astype(jnp.int32)
    send_id = jnp.sum(matches * block_id[None, :], axis=1)
    filled = jnp.sum(matches, axis=1)
    send_grid = send_id.reshape(dev_count, slots).T
    fill_grid = filled.reshape(dev_count, slots).T
    send_row = (send_grid // block_cols)[:, None, :]
    send_col = send_grid % block_cols
    send_tp = (send_col // cols_per_dev)[:, None, :]
    send_local = (send_col % cols_per_dev)[:, None, :]
    half_index = jnp.arange(halves, dtype=jnp.int32)[None, :, None]
    picked = spread[send_local, send_row, half_index, send_tp]
    outbox = jnp.where(fill_grid[:, None, :, None] > 0, picked, jnp.zeros((), jnp.bfloat16))
    inbox = move_blocks(outbox)
    grad_blocks = inbox.reshape(slots, side, side)
    myself = lax.axis_index(("shard", "tp"))
    mine = lax.dynamic_slice_in_dim(filled, myself * slots, slots)
    results = precondition_slots(
        grad_blocks, left_stat, right_stat, left_basis, right_basis, moment, second
    )
    block_updates, left_new, right_new, first_new, squares_new = results
    retain = mine[:, None, None] > 0
    new_left = jnp.where(retain, left_new, left_stat)
    new_right = jnp.where(retain, right_new, right_stat)
    new_moment = jnp.where(retain, first_new, moment)
    new_second = jnp.where(retain, squares_new, second)
    returned = move_updates(block_updates.reshape(slots, halves, dev_count, piece_len))
    block_count = table.shape[0]
    positions = jnp.arange(block_count, dtype=jnp.int32)
    block_match = (block_id[None, :] == positions[:, None]).astype(jnp.int32)
    slot_of_block = jnp.sum(block_match * state_row[None, :], axis=1)
    local_col = jnp.arange(cols_per_dev, dtype=jnp.int32)[:, None, None, None]
    row_index = jnp.arange(block_rows, dtype=jnp.int32)[None, :, None, None]
    half_grid = jnp.arange(halves, dtype=jnp.int32)[None, None, :, None]
    tp_index = jnp.arange(tp_count, dtype=jnp.int32)[None, None, None, :]
    which = row_index * block_cols + tp_index * cols_per_dev + local_col
    which = jnp.broadcast_to(which, (cols_per_dev, block_rows, halves, tp_count))
    chosen = slot_of_block[which]
    gathered = returned[chosen % slots, half_grid, chosen // slots]
    arrived = move_stripes(gathered.reshape(cols_per_dev, dev_count, piece_len))
    update = (
        arrived.reshape(cols_per_dev, row_dev, side).transpose(1, 0, 2).reshape(row_dev, col_dev)
    )
    return (update, new_left, new_right, new_moment, new_second)


def solution(mesh):
    in_specs = (
        P("shard", "tp"),
        P(),
        P(("shard", "tp"), None, None),
        P(("shard", "tp"), None, None),
        P(("shard", "tp"), None, None),
        P(("shard", "tp"), None, None),
        P(("shard", "tp"), None, None),
        P(("shard", "tp"), None, None),
    )
    out_specs = (
        P("shard", "tp"),
        P(("shard", "tp"), None, None),
        P(("shard", "tp"), None, None),
        P(("shard", "tp"), None, None),
        P(("shard", "tp"), None, None),
    )
    return jax.shard_map(shards, mesh=mesh, in_specs=in_specs, out_specs=out_specs, check_vma=False)
```

profile of v0, /device:TPU:0, one launch (start us, length us, event | category | flops | bytes accessed | tf_op | source)
XLA Modules:
  0.0 781.7 jit_solution(5679978023797544569)
XLA Ops:
  0.6 6.4 copy.88
  7.1 7.5 all-to-all-start
  15.8 92.4 %all-to-all-done = bf16[8,32,8192]{2,0,1:T(8,128)(2,1)} async-done(((bf16[8,32,8192]{2,0,1:T(8,128)(2,1)}), bf16[8,32,8192]{2,0,1:T(8,128)(2,1)}, u32[]{:S(2)}, u32[]{:S(2)}) %all-to-all-start) | async-done | bytes 4194336 | tf_op jit(solution)/shard_map/all_to_all | solution.py:22
  108.2 7.4 copy.85
  115.7 30.3 %gather_fusion = bf16[384,8192]{1,0:T(8,128)(2,1)} fusion(bf16[8,8,1,4,8192]{4,3,2,1,0:T(4,128)(2,1)} %copy.85, s32[384]{0:T(512)S(1)} %reshape.272), kind=kCustom, calls=%fused_computation | custom fusion | bytes 12589056 | tf_op jit(solution)/shard_map/gather | solution.py:99
  145.9 13.7 %copy_select_fusion = bf16[12,1,32,8192]{3,0,1,2:T(8,128)(2,1)} fusion(bf16[12,1,32,8192]{3,2,0,1:T(8,128)(2,1)} %bitcast.82, pred[12,32]{0,1:T(8,128)(4,1)S(1)} %bitcast.89), kind=kLoop, calls=%fused_computation.12 | loop fusion | flops 3145728 | bytes 12583296 | tf_op jit(solution)/shard_map/jit(_where)/select_n | solution.py:100
  164.2 185.8 %all-to-all-done.1 = bf16[12,1,32,8192]{3,0,1,2:T(8,128)(2,1)} async-done(((bf16[12,1,32,8192]{3,0,1,2:T(8,128)(2,1)}), bf16[12,1,32,8192]{3,0,1,2:T(8,128)(2,1)}, u32[]{:S(2)}, u32[]{:S(2)}) %all-to-all-start.1) | async-done | bytes 6291488 | tf_op jit(solution)/shard_map/all_to_all | solution.py:26
  350.0 9.5 %copy.67 = bf16[12,1,32,8192]{3,2,0,1:T(8,128)(2,1)} copy(bf16[12,1,32,8192]{3,0,1,2:T(8,128)(2,1)} %all-to-all-done.1) | data formatting | bytes 12582912 | tf_op jit(solution)/shard_map/all_to_all | solution.py:26
  359.5 10.4 %reshape.265 = bf16[12,512,512]{2,1,0:T(8,128)(2,1)} reshape(bf16[12,1,32,8192]{3,2,0,1:T(8,128)(2,1)} %copy.67) | data formatting | bytes 12582912 | tf_op jit(solution)/shard_map/reshape | solution.py:102
  370.0 15.1 %fusion.8 = f32[12,512,512]{2,1,0:T(8,128)} fusion(bf16[12,512,512]{2,1,0:T(8,128)(2,1)} %param.13, bf16[12,512,512]{2,1,0:T(8,128)(2,1)} %param.12, bf16[12,512,512]{2,1,0:T(8,128)(2,1)} %reshape.265, bf16[12,512,512]{2,1,0:T(8,128)(2,1)} %param.14), kind=kOutput, calls=%fused_computation.17 | convolution fusion | flops 6464471040 | bytes 37748736 | tf_op jit(solution)/shard_map/sij,sjk->sik/dot_general | solution.py:59
  385.0 22.5 %fusion.1 = (f32[12,512,512]{2,1,0:T(8,128)}, f32[12,512,512]{2,1,0:T(8,128)}) fusion(f32[12,512,512]{2,1,0:T(8,128)} %param.15, pred[12]{0:T(512)(128)(4,1)S(1)} %dynamic-slice_compare_fusion, bf16[12,512,512]{2,1,0:T(8,128)(2,1)} %param.13, bf16[12,512,512]{2,1,0:T(8,128)(2,1)} %reshape.265, bf16[12,512,512]{2,1,0:T(8,128)(2,1)} %param.12), kind=kOutput, calls=%fused_computation.9 | convolution fusion | flops 6461325312 | bytes 56623116 | tf_op jit(solution)/shard_map/sij,sjk->sik/dot_general | solution.py:58
  407.6 20.9 %fusion.10 = bf16[12,512,512]{2,1,0:T(8,128)(2,1)} fusion(bf16[12,512,512]{2,1,0:T(8,128)(2,1)} %param.12, f32[12,512,512]{2,1,0:T(8,128)} %fusion.8, f32[12,512,512]{2,1,0:T(8,128)} %get-tuple-element.17, f32[12,512,512]{2,1,0:T(8,128)} %param.15), kind=kOutput, calls=%fused_computation.20 | convolution fusion | flops 3243245568 | bytes 50331648 | tf_op jit(solution)/shard_map/sij,sjk->sik/dot_general | solution.py:62
  428.5 10.9 %fusion.12 = bf16[12,512,512]{2,1,0:T(8,128)(2,1)} fusion(bf16[12,512,512]{2,1,0:T(8,128)(2,1)} %param.13, bf16[12,512,512]{2,1,0:T(8,128)(2,1)} %fusion.10), kind=kOutput, calls=%fused_computation.22 | convolution fusion | flops 3224371200 | bytes 18874368 | tf_op jit(solution)/shard_map/sij,skj->sik/dot_general | solution.py:65
  439.4 10.4 %reshape.266 = bf16[12,1,32,8192]{3,2,0,1:T(8,128)(2,1)} reshape(bf16[12,512,512]{2,1,0:T(8,128)(2,1)} %fusion.12) | data formatting | bytes 12582912 | tf_op jit(solution)/shard_map/reshape | solution.py:114
  449.8 9.6 %copy.74 = bf16[12,1,32,8192]{3,0,1,2:T(8,128)(2,1)} copy(bf16[12,1,32,8192]{3,2,0,1:T(8,128)(2,1)} %reshape.266) | data formatting | bytes 12582912 | tf_op jit(solution)/shard_map/reshape | solution.py:114
  466.1 183.0 %all-to-all-done.2 = bf16[12,1,32,8192]{3,0,1,2:T(8,128)(2,1)} async-done(((bf16[12,1,32,8192]{3,0,1,2:T(8,128)(2,1)}), bf16[12,1,32,8192]{3,0,1,2:T(8,128)(2,1)}, u32[]{:S(2)}, u32[]{:S(2)}) %all-to-all-start.2) | async-done | bytes 6291488 | tf_op jit(solution)/shard_map/all_to_all | solution.py:30
  649.1 9.5 %copy.75 = bf16[12,1,32,8192]{3,2,1,0:T(8,128)(2,1)} copy(bf16[12,1,32,8192]{3,0,1,2:T(8,128)(2,1)} %all-to-all-done.2) | data formatting | bytes 12582912 | tf_op jit(solution)/shard_map/all_to_all | solution.py:30
  658.6 12.3 %gather_fusion.2 = bf16[256,8192]{1,0:T(8,128)(2,1)} fusion(bf16[12,1,32,8192]{3,2,1,0:T(8,128)(2,1)} %copy.75, s32[256]{0:T(256)S(1)} %reshape.288), kind=kCustom, calls=%fused_computation.2 | custom fusion | bytes 8391680 | tf_op jit(solution)/shard_map/gather | solution.py:126
  670.9 6.7 copy.76
  681.2 10.3 %broadcast_select_fusion = bf16[12,512,512]{2,1,0:T(8,128)(2,1)} fusion(bf16[12,512,512]{2,1,0:T(8,128)(2,1)} %param.14, pred[12]{0:T(512)(128)(4,1)S(1)} %dynamic-slice_compare_fusion, bf16[12,512,512]{2,1,0:T(8,128)(2,1)} %reshape.265), kind=kLoop, calls=%fused_computation.19 | loop fusion | flops 22020096 | bytes 18874380 | tf_op jit(solution)/shard_map/jit(_where)/select_n | solution.py:112
  691.5 16.0 %fusion.3 = bf16[12,512,512]{2,1,0:T(8,128)(2,1)} fusion(bf16[12,512,512]{2,1,0:T(8,128)(2,1)} %param.11, pred[12]{0:T(512)(128)(4,1)S(1)} %dynamic-slice_compare_fusion, bf16[12,512,512]{2,1,0:T(8,128)(2,1)} %reshape.265), kind=kOutput, calls=%fused_computation.11 | convolution fusion | flops 3240099840 | bytes 18874380 | tf_op jit(solution)/shard_map/ski,skj->sij/dot_general | solution.py:46
  707.5 14.6 %fusion.2 = bf16[12,512,512]{2,1,0:T(8,128)(2,1)} fusion(bf16[12,512,512]{2,1,0:T(8,128)(2,1)} %param.10, pred[12]{0:T(512)(128)(4,1)S(1)} %dynamic-slice_compare_fusion, bf16[12,512,512]{2,1,0:T(8,128)(2,1)} %reshape.265), kind=kOutput, calls=%fused_computation.10 | convolution fusion | flops 3240099840 | bytes 18874380 | tf_op jit(solution)/shard_map/sik,sjk->sij/dot_general | solution.py:41
  722.1 52.9 %all-to-all-done.3 = bf16[8,32,8192]{2,0,1:T(8,128)(2,1)} async-done(((bf16[8,32,8192]{2,0,1:T(8,128)(2,1)}), bf16[8,32,8192]{2,0,1:T(8,128)(2,1)}, u32[]{:S(2)}, u32[]{:S(2)}) %all-to-all-start.3) | async-done | bytes 4194336 | tf_op jit(solution)/shard_map/all_to_all | solution.py:34
  775.1 6.4 copy.89
  (39 shorter events, 15.9 us)
Async XLA Ops:
  7.1 7.5 copy-start
  7.1 101.2 %all-to-all-start = ((bf16[8,32,8192]{2,0,1:T(8,128)(2,1)}), bf16[8,32,8192]{2,0,1:T(8,128)(2,1)}, u32[]{:S(2)}, u32[]{:S(2)}) async-start(bf16[8,32,8192]{2,0,1:T(8,128)(2,1)} %bitcast.84), calls=%async_computation | async-start | bytes 8388608 | tf_op jit(solution)/shard_map/all_to_all | solution.py:22
  159.7 190.3 %all-to-all-start.1 = ((bf16[12,1,32,8192]{3,0,1,2:T(8,128)(2,1)}), bf16[12,1,32,8192]{3,0,1,2:T(8,128)(2,1)}, u32[]{:S(2)}, u32[]{:S(2)}) async-start(bf16[12,1,32,8192]{3,0,1,2:T(8,128)(2,1)} %copy_select_fusion), calls=%async_computation.1 | async-start | bytes 16777216 | tf_op jit(solution)/shard_map/all_to_all | solution.py:26
  459.4 189.7 %all-to-all-start.2 = ((bf16[12,1,32,8192]{3,0,1,2:T(8,128)(2,1)}), bf16[12,1,32,8192]{3,0,1,2:T(8,128)(2,1)}, u32[]{:S(2)}, u32[]{:S(2)}) async-start(bf16[12,1,32,8192]{3,0,1,2:T(8,128)(2,1)} %copy.74), calls=%async_computation.2 | async-start | bytes 16777216 | tf_op jit(solution)/shard_map/all_to_all | solution.py:30
  677.6 97.5 %all-to-all-start.3 = ((bf16[8,32,8192]{2,0,1:T(8,128)(2,1)}), bf16[8,32,8192]{2,0,1:T(8,128)(2,1)}, u32[]{:S(2)}, u32[]{:S(2)}) async-start(bf16[8,32,8192]{2,0,1:T(8,128)(2,1)} %copy.76), calls=%async_computation.3 | async-start | bytes 8388608 | tf_op jit(solution)/shard_map/all_to_all | solution.py:34
where the time goes:
time: 788 us; the launch traced here: 782 us
  waiting for transfers between devices  514 us (65%)
  local copies, waits for them, and re-layouts  122 us (15%)
  matrix products  100 us (13%)
  other arithmetic  25 us (3%)
  starting transfers between devices  19.2 us (2%)
    all_to_all x1, waiting for transfers between devices, move_blocks(): lax.all_to_all(array, ('shard', 'tp'), split_axis=2, concat_axis=2, tiled...  186 us
    all_to_all x1, waiting for transfers between devices, move_updates(): lax.all_to_all(array, ('shard', 'tp'), split_axis=2, concat_axis=2, tiled...  183 us
    all_to_all x1, waiting for transfers between devices, move_grad(): lax.all_to_all(array, ('shard', 'tp'), split_axis=1, concat_axis=1, tiled...  92.4 us
    all_to_all x1, waiting for transfers between devices, move_stripes(): lax.all_to_all(array, ('shard', 'tp'), split_axis=1, concat_axis=1, tiled...  52.9 us
    gather x1, local copies, waits for them, and re-layouts, shards(): picked = spread[send_local, send_row, half_index, send_tp]  30.3 us
    dot_general x1, matrix products, precondition_slots(): jnp.einsum('sij,sjk->sik', left_grad, right_q, preferred_element_type=jnp...  22.5 us
    dot_general x1, matrix products, precondition_slots(): jnp.einsum('sij,sjk->sik', left_q, scaled, preferred_element_type=jnp.flo...  20.9 us
    reshape x2, local copies, waits for them, and re-layouts, shards(): block_updates.reshape(slots, halves, dev_count, piece_len)  20 us
  transfers between devices with their start and end apart: 4, of which 4 were waited for; matrix products, arithmetic and copies ran while one was open for 6% of the time, Pallas kernels for 0%

commit v1 on v0

v1 whole, which is shorter than its diff:
```python
import functools

import jax
import jax.numpy as jnp
from jax import lax
from jax.experimental import pallas as pl
from jax.experimental.pallas import tpu as pltpu
from jax.sharding import PartitionSpec as P

beta_moment = 0.9
beta_second = 0.95
beta_stats = 0.95
epsilon = 1e-08
AXES = ("shard", "tp")


def slot_table(table, slots):
    owners = table[:, 2]
    count = owners.shape[0]
    order = jnp.arange(count, dtype=jnp.int32)
    earlier = (owners[None, :] == owners[:, None]) & (order[None, :] < order[:, None])
    slot_rank = jnp.sum(earlier.astype(jnp.int32), axis=1)
    return owners * slots + slot_rank


def exchange(array):
    return lax.all_to_all(array, AXES, split_axis=0, concat_axis=0, tiled=True)


def dot(a, b, dims):
    return lax.dot_general(a, b, (dims, ((), ())), preferred_element_type=jnp.float32)


def pack_kernel(group, slots, first, count, halves, tp_count, side, src_ref, col_ref, in_ref, out_ref):
    base = pl.program_id(0) * group

    def device(d, carry):
        for k in range(count):
            entry = (base + d) * slots + first + k
            src = src_ref[entry]
            col = pl.multiple_of(col_ref[entry] * side, side)
            for h in range(halves):
                out_ref[d, k, h] = in_ref[src + h * tp_count, :, pl.ds(col, side)]
        return carry

    lax.fori_loop(0, group, device, 0)


def pack(received, src, col, slots, first, count, halves, tp_count, side):
    dev_count, rows, cols = received.shape
    group = 4 if dev_count % 4 == 0 else 1
    return pl.pallas_call(
        functools.partial(pack_kernel, group, slots, first, count, halves, tp_count, side),
        grid_spec=pltpu.PrefetchScalarGridSpec(
            num_scalar_prefetch=2,
            grid=(dev_count // group,),
            in_specs=[pl.BlockSpec((dev_count, rows, cols), lambda i, *_: (0, 0, 0))],
            out_specs=pl.BlockSpec((group, count, halves, rows, side), lambda i, *_: (i, 0, 0, 0, 0)),
        ),
        out_shape=jax.ShapeDtypeStruct((dev_count, count, halves, rows, side), received.dtype),
        cost_estimate=pl.CostEstimate(flops=0, bytes_accessed=received.size * 6, transcendentals=0),
    )(src, col, received)


def unpack_kernel(group, firsts, halves, tp_count, cols_per_dev, side, own_ref, slot_ref, *refs):
    out_ref = refs[-1]
    base = pl.program_id(0) * group

    def device(d, carry):
        dev = base + d
        shard = dev // tp_count
        half = shard % halves
        place = (shard // halves * tp_count + dev % tp_count) * cols_per_dev
        for c in range(cols_per_dev):
            owner = own_ref[place + c]
            slot = slot_ref[place + c]
            value = refs[0][owner, jnp.minimum(slot, refs[0].shape[1] - 1), half]
            for ref, first in zip(refs[1:-1], firsts[1:]):
                inner = jnp.clip(slot - first, 0, ref.shape[1] - 1)
                value = jnp.where(slot >= first, ref[owner, inner, half], value)
            out_ref[d, :, c * side : (c + 1) * side] = value
        return carry

    lax.fori_loop(0, group, device, 0)


def unpack(chunks, firsts, own, slot, tp_count, cols_per_dev):
    dev_count, _, halves, rows, side = chunks[0].shape
    group = 4 if dev_count % 4 == 0 else 1
    cols = cols_per_dev * side
    return pl.pallas_call(
        functools.partial(unpack_kernel, group, firsts, halves, tp_count, cols_per_dev, side),
        grid_spec=pltpu.PrefetchScalarGridSpec(
            num_scalar_prefetch=2,
            grid=(dev_count // group,),
            in_specs=[pl.BlockSpec(c.shape, lambda i, *_: (0, 0, 0, 0, 0)) for c in chunks],
            out_specs=pl.BlockSpec((group, rows, cols), lambda i, *_: (i, 0, 0)),
        ),
        out_shape=jax.ShapeDtypeStruct((dev_count, rows, cols), chunks[0].dtype),
        cost_estimate=pl.CostEstimate(flops=0, bytes_accessed=dev_count * rows * cols * 5, transcendentals=0),
    )(own, slot, *chunks)


def slot_kernel(first, packed, mine_ref, x_ref, left, right, left_q, right_q, moment, second, *refs):
    out_ref, left_o, right_o, moment_o, second_o = refs[-5:]
    side = left.shape[-1]
    used = mine_ref[first + pl.program_id(0)] > 0

    @pl.when(used)
    def _():
        if packed:
            halves = x_ref.shape[2]
            parts = [x_ref[:, 0, h].reshape(side // halves, side) for h in range(halves)]
            grad = parts[0] if halves == 1 else jnp.concatenate(parts, axis=0)
        else:
            grad = x_ref[0]
        ql = left_q[0]
        qr = right_q[0]
        first_new = (
            beta_moment * moment[0].astype(jnp.float32)
            + (1.0 - beta_moment) * grad.astype(jnp.float32)
        ).astype(jnp.bfloat16)
        moment_o[0] = first_new
        left_grad = dot(ql, grad, ((0,), (0,))).astype(jnp.bfloat16)
        rotated = dot(left_grad, qr, ((1,), (0,)))
        squares_new = beta_second * second[0] + (1.0 - beta_second) * rotated * rotated
        second_o[0] = squares_new
        left_first = dot(ql, first_new, ((0,), (0,))).astype(jnp.bfloat16)
        first_rot = dot(left_first, qr, ((1,), (0,)))
        scaled = (first_rot / (jnp.sqrt(squares_new) + epsilon)).astype(jnp.bfloat16)
        back = dot(ql, scaled, ((1,), (0,))).astype(jnp.bfloat16)
        result = dot(back, qr, ((1,), (1,))).astype(jnp.bfloat16)
        if packed:
            halves = x_ref.shape[2]
            step = side // halves
            for h in range(halves):
                out_ref[:, 0, h] = result[h * step : (h + 1) * step].reshape(
                    x_ref.shape[0], x_ref.shape[3], side
                )
        else:
            out_ref[0] = result
        left_o[0] = (
            beta_stats * left[0].astype(jnp.float32)
            + (1.0 - beta_stats) * dot(grad, grad, ((1,), (1,)))
        ).astype(jnp.bfloat16)
        right_o[0] = (
            beta_stats * right[0].astype(jnp.float32)
            + (1.0 - beta_stats) * dot(grad, grad, ((0,), (0,)))
        ).astype(jnp.bfloat16)

    @pl.when(jnp.logical_not(used))
    def _():
        out_ref[...] = jnp.zeros_like(out_ref)
        left_o[...] = left[...]
        right_o[...] = right[...]
        moment_o[...] = moment[...]
        second_o[...] = second[...]


def precondition(x, mine, states, done, first, packed):
    left = states[0]
    slots, side, _ = left.shape
    if packed:
        dev_count, count, halves, rows, _ = x.shape
        x_spec = pl.BlockSpec((dev_count, 1, halves, rows, side), lambda i, *_: (0, i, 0, 0, 0))
    else:
        count = x.shape[0]
        x_spec = pl.BlockSpec((1, side, side), lambda i, *_: (i, 0, 0))
    state_spec = pl.BlockSpec((1, side, side), lambda i, *_: (first + i, 0, 0))
    done = list(done)
    kept = [jax.ShapeDtypeStruct(states[k].shape, states[k].dtype) for k in (0, 1, 4, 5)]
    return pl.pallas_call(
        functools.partial(slot_kernel, first, packed),
        grid_spec=pltpu.PrefetchScalarGridSpec(
            num_scalar_prefetch=1,
            grid=(count,),
            in_specs=[x_spec] + [state_spec] * 6 + [pl.BlockSpec(memory_space=pl.ANY)] * len(done),
            out_specs=[x_spec] + [state_spec] * 4,
        ),
        out_shape=[jax.ShapeDtypeStruct(x.shape, x.dtype)] + kept,
        input_output_aliases={8 + k: 1 + k for k in range(len(done))},
        cost_estimate=pl.CostEstimate(
            flops=count * 16 * side**3,
            bytes_accessed=count * side * side * 26,
            transcendentals=count * side * side,
        ),
    )(mine, x, *states, *done)


def shards(gradient, table, left_stat, right_stat, left_basis, right_basis, moment, second):
    shard_count = lax.axis_size("shard")
    tp_count = lax.axis_size("tp")
    dev_count = shard_count * tp_count
    row_dev, col_dev = gradient.shape
    slots = left_stat.shape[0]
    side = left_stat.shape[1]
    halves = side // row_dev
    cols_per_dev = col_dev // side
    block_cols = tp_count * cols_per_dev
    rows = row_dev // dev_count
    packed = rows % 16 == 0
    received = exchange(gradient.reshape(dev_count, rows, col_dev))

    state_row = slot_table(table, slots)
    block_id = table[:, 0] * block_cols + table[:, 1]
    targets = jnp.arange(dev_count * slots, dtype=jnp.int32)
    matches = (state_row[None, :] == targets[:, None]).astype(jnp.int32)
    send_id = jnp.sum(matches * block_id[None, :], axis=1)
    filled = jnp.sum(matches, axis=1)
    send_col = send_id % block_cols
    src = (send_id // block_cols) * halves * tp_count + send_col // cols_per_dev
    col = send_col % cols_per_dev
    myself = lax.axis_index(AXES)
    mine = lax.dynamic_slice_in_dim(filled, myself * slots, slots)
    positions = jnp.arange(table.shape[0], dtype=jnp.int32)
    block_match = (block_id[None, :] == positions[:, None]).astype(jnp.int32)
    slot_of_block = jnp.sum(block_match * state_row[None, :], axis=1)
    own = slot_of_block // slots
    slot = slot_of_block % slots

    half = (slots + 1) // 2
    chunks = [(0, half), (half, slots - half)] if slots > 1 else [(0, slots)]
    states = (left_stat, right_stat, left_basis, right_basis, moment, second)
    tiles = received.reshape(dev_count, rows, cols_per_dev, side)
    half_index = jnp.arange(halves, dtype=jnp.int32)
    inbox = []
    for first, count in chunks:
        if packed:
            out = pack(received, src, col, slots, first, count, halves, tp_count, side)
        else:
            src_c = src.reshape(dev_count, slots)[:, first : first + count]
            col_c = col.reshape(dev_count, slots)[:, first : first + count]
            out = tiles[src_c[:, :, None] + half_index * tp_count, :, col_c[:, :, None]]
        inbox.append(exchange(out))
    done = ()
    returned = []
    for x, (first, count) in zip(inbox, chunks):
        if not packed:
            x = x.transpose(1, 2, 0, 3, 4).reshape(count, side, side)
        update, *done = precondition(x, mine, states, done, first, packed)
        if not packed:
            update = update.reshape(count, halves, dev_count, rows, side).transpose(2, 0, 1, 3, 4)
        returned.append(exchange(update))
    if packed:
        outbox = unpack(returned, tuple(f for f, _ in chunks), own, slot, tp_count, cols_per_dev)
    else:
        back = jnp.concatenate(returned, axis=1)
        dev = jnp.arange(dev_count, dtype=jnp.int32)[:, None]
        place = (dev // tp_count // halves * tp_count + dev % tp_count) * cols_per_dev
        place = place + jnp.arange(cols_per_dev, dtype=jnp.int32)[None, :]
        picked = back[own[place], slot[place], dev // tp_count % halves]
        outbox = picked.transpose(0, 2, 1, 3).reshape(dev_count, rows, col_dev)
    update = exchange(outbox).reshape(row_dev, col_dev)
    new_left, new_right, new_moment, new_second = done
    return (update, new_left, new_right, new_moment, new_second)


def solution(mesh):
    state = P(AXES, None, None)
    in_specs = (P("shard", "tp"), P()) + (state,) * 6
    out_specs = (P("shard", "tp"),) + (state,) * 4
    return jax.shard_map(shards, mesh=mesh, in_specs=in_specs, out_specs=out_specs, check_vma=False)
```

time: 788 us -> 521 us (0.66)
  waiting for transfers between devices: 514 us -> 331 us
  local copies, waits for them, and re-layouts: 122 us -> 6 us
  matrix products: 100 us -> 0 us
  blocking collectives: 0 us -> 97.7 us
  Pallas kernels: 0 us -> 60.2 us
  other arithmetic: 25 us -> 1.7 us
    all_to_all x4 -> x5, waiting for transfers between devices: 514 us -> 331 us  [exchange(): return lax.all_to_all(array, AXES, split_axis=0, concat_axis=0, tiled=True)]
    dot_general x6 -> x0, matrix products: 100 us -> none  [the longest x1 22.5 us: precondition_slots(): jnp.einsum('sij,sjk->sik', left_grad, right_q, preferred_element_type=jnp...]
    all_to_all x0 -> x1, blocking collectives: none -> 97.7 us  [exchange(): return lax.all_to_all(array, AXES, split_axis=0, concat_axis=0, tiled=True)]
    pallas_call x0 -> x5, Pallas kernels: none -> 60.2 us  [the longest x2 39.6 us: precondition(): pl.pallas_call(functools.partial(slot_kernel, first, packed), grid_spec=p...]
    gather x3 -> x0, local copies, waits for them, and re-layouts: 44.7 us -> none  [the longest x1 30.3 us: shards(): picked = spread[send_local, send_row, half_index, send_tp]]
    reshape x6 -> x0, local copies, waits for them, and re-layouts: 44.6 us -> none  [the longest x2 20 us: shards(): block_updates.reshape(slots, halves, dev_count, piece_len)]
    select_n x4 -> x2, other arithmetic: 24 us -> 1.19 us  [the longest x1 0.6 us: shards(): col = send_col % cols_per_dev]
    all_to_all x2 -> x0, local copies, waits for them, and re-layouts: 19.1 us -> none  [the longest x1 9.53 us: move_blocks(): lax.all_to_all(array, ('shard', 'tp'), split_axis=2, concat_axis=2, tiled...]
  transfers between devices with their start and end apart: 4 -> 5, of which waited for: 4 -> 5; matrix products, arithmetic and copies ran while one was open for 6% -> 0% of each run, Pallas kernels for 0% -> 9%
where the time goes in v1:
time: 521 us
  waiting for transfers between devices  331 us (64%)
  blocking collectives  97.7 us (19%)
  Pallas kernels  60.2 us (12%)
  starting transfers between devices  23.8 us (5%)
  local copies, waits for them, and re-layouts  6 us (1%)
    all_to_all x5, waiting for transfers between devices, exchange(): return lax.all_to_all(array, AXES, split_axis=0, concat_axis=0, tiled=True)  331 us
    all_to_all x1, blocking collectives, exchange(): return lax.all_to_all(array, AXES, split_axis=0, concat_axis=0, tiled=True)  97.7 us
    pallas_call x2, Pallas kernels, precondition(): pl.pallas_call(functools.partial(slot_kernel, first, packed), grid_spec=p...  39.6 us
    all_to_all x5, starting transfers between devices, exchange(): return lax.all_to_all(array, AXES, split_axis=0, concat_axis=0, tiled=True)  23.8 us
    pallas_call x2, Pallas kernels, pack(): pl.pallas_call(functools.partial(pack_kernel, group, slots, first, count,...  12.6 us
  transfers between devices with their start and end apart: 5, of which 5 were waited for; matrix products, arithmetic and copies ran while one was open for 0% of the time, Pallas kernels for 9%

profile of v1, /device:TPU:0, one launch (start us, length us, event | category | flops | bytes accessed | tf_op | source)
XLA Modules:
  0.0 520.7 jit_solution(12106552861633704672)
XLA Ops:
  0.6 7.5 %all-to-all-start = ((bf16[32,16,4096]{2,1,0:T(8,128)(2,1)}), bf16[32,16,4096]{2,1,0:T(8,128)(2,1)}, u32[]{:S(2)}, u32[]{:S(2)}) async-start(bf16[32,16,4096]{2,1,0:T(8,128)(2,1)} %bitcast.5), calls=%async_computation | async-start | bytes 8388608 | tf_op jit(solution)/shard_map/all_to_all | solution.py:27
  8.1 0.2 convert_reduce_fusion.1
  8.3 0.2 select_reduce_fusion
  8.5 0.6 add_select_fusion
  9.1 92.7 %all-to-all-done.in_ref = bf16[32,16,4096]{2,1,0:T(8,128)(2,1)} async-done(((bf16[32,16,4096]{2,1,0:T(8,128)(2,1)}), bf16[32,16,4096]{2,1,0:T(8,128)(2,1)}, u32[]{:S(2)}, u32[]{:S(2)}) %all-to-all-start) | async-done | bytes 4194336 | tf_op jit(solution)/shard_map/all_to_all | solution.py:27
  101.8 6.3 %shard_map.119 = bf16[32,6,1,16,512]{4,3,2,1,0:T(8,128)(2,1)} custom-call(s32[384]{0:T(512)} %get-tuple-element.30.src_ref, s32[384]{0:T(512)} %get-tuple-element.29.col_ref, bf16[32,16,4096]{2,1,0:T(8,128)(2,1)} %all-to-all-done.in_ref), custom_call_target="tpu_custom_call" | custom-call | bytes 12582912 | tf_op jit(solution)/shard_map/pallas_call | solution.py:52
  108.1 4.1 all-to-all-start.1
  112.2 6.3 %shard_map.121 = bf16[32,6,1,16,512]{4,3,2,1,0:T(8,128)(2,1)} custom-call(s32[384]{0:T(512)} %get-tuple-element.30.src_ref, s32[384]{0:T(512)} %get-tuple-element.29.col_ref, bf16[32,16,4096]{2,1,0:T(8,128)(2,1)} %all-to-all-done.in_ref), custom_call_target="tpu_custom_call" | custom-call | bytes 12582912 | tf_op jit(solution)/shard_map/pallas_call | solution.py:52
  118.6 65.0 %all-to-all-done.1.x_ref = bf16[32,6,1,16,512]{4,3,2,1,0:T(8,128)(2,1)S(1)} async-done(((bf16[32,6,1,16,512]{4,3,2,1,0:T(8,128)(2,1)}), bf16[32,6,1,16,512]{4,3,2,1,0:T(8,128)(2,1)S(1)}, u32[]{:S(2)}, u32[]{:S(2)}) %all-to-all-start.1) | async-done | bytes 3145760 | tf_op jit(solution)/shard_map/all_to_all | solution.py:27
  183.6 1.7 copy-done.2
  185.2 4.0 all-to-all-start.3
  189.3 0.6 dynamic_slice.3.mine_ref
  189.9 21.9 %shard_map.120 = (bf16[32,6,1,16,512]{4,3,2,1,0:T(8,128)(2,1)}, bf16[12,512,512]{2,1,0:T(8,128)(2,1)}, bf16[12,512,512]{2,1,0:T(8,128)(2,1)}, bf16[12,512,512]{2,1,0:T(8,128)(2,1)}, f32[12,512,512]{2,1,0:T(8,128)}) custom-call(s32[12]{0:T(128)} %dynamic_slice.3.mine_ref, bf16[32,6,1,16,512]{4,3,2,1,0:T(8,128)(2,1)} %copy-done.2, bf16[12,512,512]{2,1,0:T(8,128)(2,1)} %left.3, ...), custom_call_target="tpu_custom_call" | custom-call | flops 12884901888 | bytes 40894464 | tf_op jit(solution)/shard_map/pallas_call | solution.py:172
  211.8 48.8 %all-to-all-done.3.x_ref = bf16[32,6,1,16,512]{4,3,2,1,0:T(8,128)(2,1)S(1)} async-done(((bf16[32,6,1,16,512]{4,3,2,1,0:T(8,128)(2,1)}), bf16[32,6,1,16,512]{4,3,2,1,0:T(8,128)(2,1)S(1)}, u32[]{:S(2)}, u32[]{:S(2)}) %all-to-all-start.3) | async-done | bytes 3145760 | tf_op jit(solution)/shard_map/all_to_all | solution.py:27
  260.6 4.1 all-to-all-start.2
  264.8 17.7 %shard_map.122 = (bf16[32,6,1,16,512]{4,3,2,1,0:T(8,128)(2,1)}, bf16[12,512,512]{2,1,0:T(8,128)(2,1)}, bf16[12,512,512]{2,1,0:T(8,128)(2,1)}, bf16[12,512,512]{2,1,0:T(8,128)(2,1)}, f32[12,512,512]{2,1,0:T(8,128)}) custom-call(s32[12]{0:T(128)} %dynamic_slice.3.mine_ref, ...), custom_call_target="tpu_custom_call", output_to_operand_aliasing={{1}: (8, {}), {2}: (9, {}), {3}: (10, {}), {4}: (11, {})} | custom-call | flops 12884901888 | bytes 40894464 | tf_op jit(solution)/shard_map/pallas_call | solution.py:172
  282.5 53.6 %all-to-all-done.2.refs_0_ = bf16[32,6,1,16,512]{4,3,2,1,0:T(8,128)(2,1)} async-done(((bf16[32,6,1,16,512]{4,3,2,1,0:T(8,128)(2,1)}), bf16[32,6,1,16,512]{4,3,2,1,0:T(8,128)(2,1)}, u32[]{:S(2)}, u32[]{:S(2)}) %all-to-all-start.2) | async-done | bytes 3145760 | tf_op jit(solution)/shard_map/all_to_all | solution.py:27
  336.1 4.0 all-to-all-start.4
  340.2 0.6 and_select_fusion
  340.8 70.6 %all-to-all-done.4.refs_1_ = bf16[32,6,1,16,512]{4,3,2,1,0:T(8,128)(2,1)S(1)} async-done(((bf16[32,6,1,16,512]{4,3,2,1,0:T(8,128)(2,1)}), bf16[32,6,1,16,512]{4,3,2,1,0:T(8,128)(2,1)S(1)}, u32[]{:S(2)}, u32[]{:S(2)}) %all-to-all-start.4) | async-done | bytes 3145760 | tf_op jit(solution)/shard_map/all_to_all | solution.py:27
  411.5 1.7 copy-done.1
  413.1 7.9 %shard_map.123 = bf16[32,16,4096]{2,1,0:T(8,128)(2,1)} custom-call(s32[256]{0:T(256)} %get-tuple-element.32.own_ref, s32[256]{0:T(256)} %get-tuple-element.31.slot_ref, bf16[32,6,1,16,512]{4,3,2,1,0:T(8,128)(2,1)} %all-to-all-done.2.refs_0_, bf16[32,6,1,16,512]{4,3,2,1,0:T(8,128)(2,1)} %copy-done.1), custom_call_target="tpu_custom_call" | custom-call | bytes 10485760 | tf_op jit(solution)/shard_map/pallas_call | solution.py:91
  421.1 97.7 %all_to_all.30 = bf16[32,16,4096]{2,1,0:T(8,128)(2,1)S(1)} all-to-all(bf16[32,16,4096]{2,1,0:T(8,128)(2,1)} %shard_map.123), channel_id=1, replica_groups=mesh['shard'=8,'tp'=4] {'shard','tp'}, dimensions={0} | all-to-all | bytes 8388608 | tf_op jit(solution)/shard_map/all_to_all | solution.py:27
  518.7 2.0 copy.22
  (9 shorter events, 0.1 us)
Async XLA Ops:
  0.6 7.5 %copy-start.3 = (s32[256,3]{0,1:T(4,128)S(1)}, s32[256,3]{0,1:T(4,128)}, u32[]{:S(2)}) copy-start(s32[256,3]{0,1:T(4,128)} %param.9) | copy-start | bytes 9220
  0.6 101.2 %all-to-all-start = ((bf16[32,16,4096]{2,1,0:T(8,128)(2,1)}), bf16[32,16,4096]{2,1,0:T(8,128)(2,1)}, u32[]{:S(2)}, u32[]{:S(2)}) async-start(bf16[32,16,4096]{2,1,0:T(8,128)(2,1)} %bitcast.5), calls=%async_computation | async-start | bytes 8388608 | tf_op jit(solution)/shard_map/all_to_all | solution.py:27
  108.1 75.5 %all-to-all-start.1 = ((bf16[32,6,1,16,512]{4,3,2,1,0:T(8,128)(2,1)}), bf16[32,6,1,16,512]{4,3,2,1,0:T(8,128)(2,1)S(1)}, u32[]{:S(2)}, u32[]{:S(2)}) async-start(bf16[32,6,1,16,512]{4,3,2,1,0:T(8,128)(2,1)} %shard_map.119), calls=%async_computation.1 | async-start | bytes 6291456 | tf_op jit(solution)/shard_map/all_to_all | solution.py:27
  183.6 1.7 copy-start.2
  185.2 75.4 %all-to-all-start.3 = ((bf16[32,6,1,16,512]{4,3,2,1,0:T(8,128)(2,1)}), bf16[32,6,1,16,512]{4,3,2,1,0:T(8,128)(2,1)S(1)}, u32[]{:S(2)}, u32[]{:S(2)}) async-start(bf16[32,6,1,16,512]{4,3,2,1,0:T(8,128)(2,1)} %shard_map.121), calls=%async_computation.3 | async-start | bytes 6291456 | tf_op jit(solution)/shard_map/all_to_all | solution.py:27
  260.6 4.2 copy-start
  260.6 75.5 %all-to-all-start.2 = ((bf16[32,6,1,16,512]{4,3,2,1,0:T(8,128)(2,1)}), bf16[32,6,1,16,512]{4,3,2,1,0:T(8,128)(2,1)}, u32[]{:S(2)}, u32[]{:S(2)}) async-start(bf16[32,6,1,16,512]{4,3,2,1,0:T(8,128)(2,1)} %get-tuple-element.15), calls=%async_computation.2 | async-start | bytes 6291456 | tf_op jit(solution)/shard_map/all_to_all | solution.py:27
  336.1 75.4 %all-to-all-start.4 = ((bf16[32,6,1,16,512]{4,3,2,1,0:T(8,128)(2,1)}), bf16[32,6,1,16,512]{4,3,2,1,0:T(8,128)(2,1)S(1)}, u32[]{:S(2)}, u32[]{:S(2)}) async-start(bf16[32,6,1,16,512]{4,3,2,1,0:T(8,128)(2,1)} %get-tuple-element.20), calls=%async_computation.4 | async-start | bytes 6291456 | tf_op jit(solution)/shard_map/all_to_all | solution.py:27
  411.5 1.7 copy-start.1
